TPU v7x, 512 devices: a whole 4x8x8 slice. The times are simulated.
512 devices in a mesh: row: 32 (over x_lo, y, core), col: 16 (over z, x_hi).
Axes of the slice: x: 4 (x_hi: 2, x_lo: 2; x = x_hi * 2 + x_lo), y: 8, z: 8, core: 2. Of those that a mesh axis runs over, the one named last changes fastest.
Arguments:
- x_slab: float32 [8192, 4096], P('col', 'row'), may hold values from -5400 to 5400, as said below
- weight_c: float32 [1], replicated, may hold values from 2048 to 16384
Outputs:
- trailing: float32 [4096, 4096], P('row', 'col')
- panels: float32 [4096, 512], P('row')
- inverses: float32 [2, 256, 256], replicated
- frobenius: float32 [1], replicated
Inputs may be any that keep to these rules, and one draw needn't show every extreme that they name: `x_slab`: real-valued entries.
All inputs are finite; a program needn't handle non-finite values.
Results may differ from a plain program's by a relative error of at most 0.00015.
Values sent between devices are 32-bit elements; how exact they have to be, the bound alone decides.
A program may use at most 64 MiB of HBM per device.

v0:
```python
import jax
import jax.numpy as jnp
from jax import lax
from jax.sharding import Mesh
from jax.sharding import PartitionSpec as P

PANEL = 256
COL = ("col_0", "col_1")
ROW = ("row_0", "row_1", "row_2")
ROW_COL = ("row_0", "row_1", "row_2", "col_0", "col_1")
HIGH = lax.Precision.HIGHEST


def broadcast(x, axis, root):
    return lax.dynamic_index_in_dim(lax.all_gather(x, axis), root, 0, keepdims=False)


def split_up(x, dim, size):
    dims = x.shape
    blocks = x.reshape(*dims[:dim], size, dims[dim] // size, *dims[dim + 1 :])
    return jnp.moveaxis(blocks, dim, 0)


def summed_on_arrival(x, axis, dim):
    blocks = split_up(x, dim, lax.axis_size(axis))
    arrived = lax.all_to_all(blocks, axis, split_axis=0, concat_axis=0, tiled=True)
    return arrived.sum(axis=0)


def rows_for(lines, size):
    spare = -len(lines) % size
    return jnp.pad(lines, [(0, spare)] + [(0, 0)] * (lines.ndim - 1))


def joined_along(blocks, dim):
    blocks = jnp.moveaxis(blocks, 0, dim)
    dims = blocks.shape
    return blocks.reshape(*dims[:dim], dims[dim] * dims[dim + 1], *dims[dim + 2 :])


def from_everyone(x, axis):
    size = lax.axis_size(axis)
    return lax.all_to_all(jnp.broadcast_to(x[None], (size, *x.shape)), axis, 0, 0, tiled=True)


def collect(x, axis, dim):
    return joined_along(from_everyone(x, axis), dim)


def sum_by_parts(x, axes):
    lines = x.reshape(-1, x.shape[-1])
    own = summed_on_arrival(rows_for(lines, lax.axis_size(axes)), axes, 0)
    whole = collect(own, axes, 0)
    return whole[: len(lines)].reshape(x.shape)


def by_axis(x, axes):
    for axis in axes:
        x = lax.psum(x, axis)
    return x


def nested_sum(x, axes):
    own = summed_on_arrival(rows_for(x, lax.axis_size(axes)), axes, 0)
    whole = collect(own, axes, 0)
    return whole[: len(x)].reshape(x.shape)


def packed_total(arrays, axis):
    ends = [0]
    for a in arrays:
        ends.append(ends[-1] + a.size)
    subtotal = nested_sum(jnp.concatenate([a.ravel() for a in arrays]), axis)
    return tuple((subtotal[b:e].reshape(a.shape) for a, b, e in zip(arrays, ends, ends[1:])))


def product(left, right):
    return jnp.dot(left, right, preferred_element_type=jnp.float32, precision=HIGH)


def invert_lower(block):
    factor = jnp.linalg.cholesky(block)
    identity = jnp.eye(block.shape[0], dtype=block.dtype)
    return lax.linalg.triangular_solve(factor, identity, left_side=True, lower=True)


def lower_panel(column, inverse, start, row_ids, panel_size):
    values = product(column, inverse.T)
    targets = start + jnp.arange(panel_size, dtype=jnp.int32)
    return jnp.where(row_ids[:, None] >= targets[None, :], values, jnp.zeros_like(values))


def panel_column(matrix, number, panel_size, tile_cols):
    owner = number * panel_size // tile_cols
    return broadcast(matrix, COL, owner)


def pick_rows(values, start, row_ids, panel_size):
    targets = start + jnp.arange(panel_size, dtype=jnp.int32)
    selector = (targets[:, None] == row_ids[None, :]).astype(jnp.float32)
    return product(selector, values)


def diagonal_block(column, start, row_ids, panel_size):
    return sum_by_parts(pick_rows(column, start, row_ids, panel_size), ROW)


def on_device(x_slab, weight_c):
    local_cols = x_slab.shape[1]
    width = local_cols * lax.axis_size(ROW)
    tile_cols = width // lax.axis_size(COL)
    panel_size = PANEL
    row_ids = lax.axis_index(ROW) * local_cols + jnp.arange(local_cols, dtype=jnp.int32)
    col_ids = lax.axis_index(COL) * tile_cols + jnp.arange(tile_cols, dtype=jnp.int32)
    squares = by_axis(jnp.sum(x_slab * x_slab), ROW_COL)
    factor_c = weight_c[0] / squares
    partial_value = lax.dot_general(
        x_slab,
        lax.all_gather(x_slab, ROW, axis=1, tiled=True),
        (((0,), (0,)), ((), ())),
        precision=HIGH,
        preferred_element_type=jnp.float32,
    )
    block = summed_on_arrival(partial_value, COL, 1)
    gram = block * factor_c + (row_ids[:, None] == col_ids[None, :]).astype(jnp.float32)
    column_one = panel_column(gram, 0, panel_size, tile_cols)
    column_two = panel_column(gram, 1, panel_size, tile_cols)
    inverse_one = invert_lower(diagonal_block(column_one, 0, row_ids, panel_size))
    lower_one = lower_panel(column_one, inverse_one, 0, row_ids, panel_size)
    raw_block, crossing = packed_total(
        (
            pick_rows(column_two, panel_size, row_ids, panel_size),
            pick_rows(lower_one, panel_size, row_ids, panel_size),
        ),
        ROW,
    )
    inverse_two = invert_lower(raw_block - product(crossing, crossing.T))
    lower_two = lower_panel(
        column_two - product(lower_one, crossing.T), inverse_two, panel_size, row_ids, panel_size
    )
    both = jnp.concatenate([lower_one, lower_two], axis=1)
    gathered = lax.all_gather(both, ROW, axis=0, tiled=True)
    mine = lax.dynamic_slice_in_dim(gathered, lax.axis_index(COL) * tile_cols, tile_cols, 0)
    matrix = gram - product(both, mine.T)
    inverses = [inverse_one, inverse_two]
    return (matrix, both, jnp.stack(inverses), jnp.sqrt(squares).reshape(1))


def solution(mesh):
    split = Mesh(mesh.devices.reshape(2, 8, 2, 8, 2), ("row_0", "row_1", "row_2", "col_0", "col_1"))
    in_specs = (P(COL, ROW), P())
    out_specs = (P(ROW, COL), P(ROW, None), P(), P())
    return jax.shard_map(
        on_device, mesh=split, in_specs=in_specs, out_specs=out_specs, check_vma=False
    )
```

profile of v0, /device:TPU:1, one launch (start us, length us, event | category | flops | bytes accessed | tf_op | source)
XLA Modules:
  0.0 585.1 jit_solution(13100792732569455945)
XLA Ops:
  7.2 0.7 all-gather.4.cloned.1.call-update
  7.9 98.4 %all-gather.4.cloned.1.call-done = f32[512,4096]{1,0:T(8,128)} async-done(((f32[512,128]{1,0:T(8,128)}), f32[512,4096]{1,0:T(8,128)}) %all-gather.4.cloned.1.call-update) | async-done | bytes 8388624 | tf_op jit(solution)/shard_map/all_gather | solution.py:119
  106.3 6.9 %fusion.41 = f32[128,4096]{1,0:T(8,128)S(1)} fusion(f32[512,128]{1,0:T(8,128)} %param.5, f32[512,4096]{1,0:T(8,128)} %all-gather.4.cloned.1.call-done), kind=kOutput, calls=%fused_computation.97 | convolution fusion | flops 3221225472 | bytes 10747904 | tf_op jit(solution)/shard_map/dot_general | solution.py:117
  113.2 1.6 copy.21
  114.8 9.5 %all-to-all-start = ((f32[16,128,256]{2,1,0:T(8,128)}), f32[16,128,256]{2,1,0:T(8,128)S(1)}, u32[]{:S(2)}, u32[]{:S(2)}) async-start(f32[16,128,256]{2,1,0:T(8,128)} %bitcast.100), calls=%async_computation | async-start | bytes 4194304 | tf_op jit(solution)/shard_map/all_to_all | solution.py:26
  124.4 0.7 multiply_reduce_fusion
  125.0 4.4 psum.35
  129.4 15.1 %psum.36 = f32[]{:T(128)} all-reduce(f32[]{:T(128)} %psum.35), channel_id=1, replica_groups=mesh['row_0'=2,'row_1'=8,'row_2'=2,'col_0'=8,'col_1'=2] {'row_1'}, use_global_device_ids=true, to_apply=%region_3.0 | all-reduce | flops 1 | bytes 8 | tf_op jit(solution)/shard_map/psum | solution.py:59
  144.5 6.4 %psum.37 = f32[]{:T(128)} all-reduce(f32[]{:T(128)} %psum.36), channel_id=1, replica_groups=mesh['row_0'=2,'row_1'=8,'row_2'=2,'col_0'=8,'col_1'=2] {'row_2'}, use_global_device_ids=true, to_apply=%region_4.0 | all-reduce | flops 1 | bytes 8 | tf_op jit(solution)/shard_map/psum | solution.py:59
  151.0 28.8 %psum.38 = f32[]{:T(128)} all-reduce(f32[]{:T(128)} %psum.37), channel_id=1, replica_groups=mesh['row_0'=2,'row_1'=8,'row_2'=2,'col_0'=8,'col_1'=2] {'col_0'}, use_global_device_ids=true, to_apply=%region_5.0 | all-reduce | flops 1 | bytes 8 | tf_op jit(solution)/shard_map/psum | solution.py:59
  179.8 5.9 %psum.39 = f32[]{:T(128)} all-reduce(f32[]{:T(128)} %psum.38), channel_id=1, replica_groups=mesh['row_0'=2,'row_1'=8,'row_2'=2,'col_0'=8,'col_1'=2] {'col_1'}, use_global_device_ids=true, to_apply=%region_6.0 | all-reduce | flops 1 | bytes 8 | tf_op jit(solution)/shard_map/psum | solution.py:59
  187.1 0.7 bitcast_add_fusion.2
  187.9 90.3 %all-gather.6.cloned.1.call-done = f32[16,128,256]{2,1,0:T(8,128)} async-done(((f32[1,128,256]{2,1,0:T(8,128)}), f32[16,128,256]{2,1,0:T(8,128)}) %all-gather.6.cloned.1.call-update) | async-done | bytes 2097168 | tf_op jit(solution)/shard_map/all_gather | solution.py:15
  278.2 1.2 fusion.10
  279.4 22.4 %all_to_all.30 = f32[32,8,256]{2,1,0:T(8,128)S(1)} all-to-all(f32[32,8,256]{2,1,0:T(8,128)S(1)} %fusion.10), channel_id=1, replica_groups=mesh['row_0'=2,'row_1'=8,'row_2'=2,'col_0'=8,'col_1'=2] {'row_0','row_1'..., dimensions={0} | all-to-all | bytes 524288 | tf_op jit(solution)/shard_map/all_to_all | solution.py:26
  301.8 0.7 broadcast_in_dim.4
  302.5 5.8 all-to-all-start.2
  308.4 1.2 fusion.8
  309.7 10.4 %all-to-all-done.2 = f32[32,8,256]{2,1,0:T(8,128)S(1)} async-done(((f32[32,8,256]{2,1,0:T(8,128)}), f32[32,8,256]{2,1,0:T(8,128)S(1)}, u32[]{:S(2)}, u32[]{:S(2)}) %all-to-all-start.2) | async-done | bytes 262176 | tf_op jit(solution)/shard_map/all_to_all | solution.py:43
  320.3 11.7 %cholesky.130 = f32[128,128]{1,0:T(8,128)S(1)} custom-call(f32[128,128]{1,0:T(8,128)S(1)} %cholesky.194), custom_call_target="Cholesky" | custom-call | tf_op jit(solution)/shard_map/jit(cholesky)/cholesky | solution.py:82
  332.1 9.8 %custom-call.13 = f32[1,128,128]{1,2,0:T(8,128)S(1)} custom-call(f32[1,128,128]{2,1,0:T(8,128)S(1)} %get-tuple-element.51), custom_call_target="InvertDiagBlocksLowerTriangular" | custom-call | tf_op jit(solution)/shard_map/jit(cholesky)/cholesky | solution.py:82
  342.4 11.7 %cholesky.147 = f32[128,128]{1,0:T(8,128)S(1)} custom-call(f32[128,128]{1,0:T(8,128)S(1)} %convolution_subtract_fusion.6), custom_call_target="Cholesky" | custom-call | tf_op jit(solution)/shard_map/jit(cholesky)/cholesky | solution.py:82
  354.2 0.6 compare_reduce_fusion.2
  356.2 4.0 while.4
  356.3 0.6 fusion.61
  356.8 1.4 bitcast_dynamic-update-slice_fusion.4
  358.8 1.4 bitcast_dynamic-update-slice_fusion.4
  360.2 31.8 %custom-call.14 = f32[2,128,128]{1,2,0:T(8,128)S(1)} custom-call(f32[2,128,128]{2,1,0:T(8,128)S(1)} %get-tuple-element.20), custom_call_target="InvertDiagBlocksLowerTriangular" | custom-call | tf_op jit(solution)/shard_map/triangular_solve/custom-call.0 | solution.py:84
  393.0 1.3 convolution_select_fusion.1
  395.3 21.0 %all_to_all.31 = f32[32,1,4096]{2,1,0:T(1,128)S(1)} all-to-all(f32[32,1,4096]{2,1,0:T(1,128)S(1)} %all_to_all.22), channel_id=1, replica_groups=mesh['row_0'=2,'row_1'=8,'row_2'=2,'col_0'=8,'col_1'=2] {'row_0','row_1'..., dimensions={0} | all-to-all | bytes 1048576 | tf_op jit(solution)/shard_map/all_to_all | solution.py:26
  416.6 1.3 broadcast_in_dim.5
  417.8 5.6 all-to-all-start.4
  423.5 16.7 %all-to-all-done.4 = f32[32,1,4096]{2,1,0:T(1,128)S(1)} async-done(((f32[32,1,4096]{2,1,0:T(1,128)}), f32[32,1,4096]{2,1,0:T(1,128)S(1)}, u32[]{:S(2)}, u32[]{:S(2)}) %all-to-all-start.4) | async-done | bytes 524320 | tf_op jit(solution)/shard_map/all_to_all | solution.py:43
  440.2 1.3 slice_reduce_fusion
  442.4 11.7 %cholesky.164 = f32[128,128]{1,0:T(8,128)S(1)} custom-call(f32[128,128]{1,0:T(8,128)S(1)} %cholesky.197), custom_call_target="Cholesky" | custom-call | tf_op jit(solution)/shard_map/jit(cholesky)/cholesky | solution.py:82
  454.1 9.8 %custom-call.15 = f32[1,128,128]{1,2,0:T(8,128)S(1)} custom-call(f32[1,128,128]{2,1,0:T(8,128)S(1)} %get-tuple-element.47), custom_call_target="InvertDiagBlocksLowerTriangular" | custom-call | tf_op jit(solution)/shard_map/jit(cholesky)/cholesky | solution.py:82
  464.4 11.8 %cholesky.181 = f32[128,128]{1,0:T(8,128)S(1)} custom-call(f32[128,128]{1,0:T(8,128)S(1)} %convolution_subtract_fusion.5), custom_call_target="Cholesky" | custom-call | tf_op jit(solution)/shard_map/jit(cholesky)/cholesky | solution.py:82
  476.3 0.6 compare_reduce_fusion
  476.9 0.6 compare_reduce_fusion.1
  478.9 4.0 while.5
  479.5 1.4 bitcast_dynamic-update-slice_fusion.5
  481.5 1.4 bitcast_dynamic-update-slice_fusion.5
  482.9 19.7 %custom-call.16 = f32[2,128,128]{1,2,0:T(8,128)S(1)} custom-call(f32[2,128,128]{2,1,0:T(8,128)S(1)} %get-tuple-element.21), custom_call_target="InvertDiagBlocksLowerTriangular" | custom-call | tf_op jit(solution)/shard_map/triangular_solve/custom-call.0 | solution.py:84
  503.5 1.3 convolution_subtract_fusion.2
  505.2 0.7 pad_maximum_fusion.4
  506.7 0.8 pad_maximum_fusion.1
  507.5 67.3 %all-gather.8.cloned.1.call-done = f32[4096,512]{1,0:T(8,128)} async-done(((f32[128,512]{1,0:T(8,128)}), f32[4096,512]{1,0:T(8,128)}) %all-gather.8.cloned.1.call-update) | async-done | bytes 8388624 | tf_op jit(solution)/shard_map/all_gather | solution.py:142
  574.8 2.4 convolution_subtract_fusion.1
  (65 shorter events, 8.0 us)
Async XLA Ops:
  7.2 99.1 %all-gather.4.cloned.1.call-start = ((), (), s32[]{:S(2)}) async-start(), calls=%async_computation.5 | async-start | bytes 8650752 | tf_op jit(solution)/shard_map/all_gather | solution.py:119
  114.8 9.6 %copy-start.1 = (f32[512,128]{1,0:T(8,128)S(1)}, f32[512,128]{1,0:T(8,128)}, u32[]{:S(2)}) copy-start(f32[512,128]{1,0:T(8,128)} %param.5) | copy-start | bytes 786436
  114.8 72.2 %all-to-all-start = ((f32[16,128,256]{2,1,0:T(8,128)}), f32[16,128,256]{2,1,0:T(8,128)S(1)}, u32[]{:S(2)}, u32[]{:S(2)}) async-start(f32[16,128,256]{2,1,0:T(8,128)} %bitcast.100), calls=%async_computation | async-start | bytes 4194304 | tf_op jit(solution)/shard_map/all_to_all | solution.py:26
  124.3 153.9 %all-gather.6.cloned.1.call-start = ((), (), s32[]{:S(2)}) async-start(), calls=%async_computation.6 | async-start | bytes 2228224 | tf_op jit(solution)/shard_map/all_gather | solution.py:15
  302.5 17.6 %all-to-all-start.2 = ((f32[32,8,256]{2,1,0:T(8,128)}), f32[32,8,256]{2,1,0:T(8,128)S(1)}, u32[]{:S(2)}, u32[]{:S(2)}) async-start(f32[32,8,256]{2,1,0:T(8,128)} %broadcast_in_dim.4), calls=%async_computation.2 | async-start | bytes 524288 | tf_op jit(solution)/shard_map/all_to_all | solution.py:43
  417.8 22.3 %all-to-all-start.4 = ((f32[32,1,4096]{2,1,0:T(1,128)}), f32[32,1,4096]{2,1,0:T(1,128)S(1)}, u32[]{:S(2)}, u32[]{:S(2)}) async-start(f32[32,1,4096]{2,1,0:T(1,128)} %broadcast_in_dim.5), calls=%async_computation.4 | async-start | bytes 1048576 | tf_op jit(solution)/shard_map/all_to_all | solution.py:43
  423.5 151.4 %all-gather.8.cloned.1.call-start = ((), (), s32[]{:S(2)}) async-start(), calls=%async_computation.7 | async-start | bytes 8650752 | tf_op jit(solution)/shard_map/all_gather | solution.py:142
  506.0 68.9 %copy-start = (f32[128,512]{1,0:T(8,128)S(1)}, f32[128,512]{1,0:T(8,128)}, u32[]{:S(2)}) copy-start(f32[128,512]{1,0:T(8,128)} %pad_maximum_fusion.4) | copy-start | bytes 786436
Sparse Core Ops, SparseCore 0:
  10.0 96.2 all-gather.3
  188.0 90.1 all-gather.5
  506.1 68.6 all-gather.7
where the time goes:
time: 590 us; the launch traced here: 585 us
  waiting for transfers between devices  284 us (48%)
  other arithmetic  124 us (21%)
  blocking collectives  104 us (18%)
  starting transfers between devices  21.1 us (4%)
  between operations  20.1 us (3%)
  matrix products  18.1 us (3%)
  local copies, waits for them, and re-layouts  14.1 us (2%)
    all_gather x1, waiting for transfers between devices, on_device(): lax.all_gather(x_slab, ROW, axis=1, tiled=True)  98.4 us
    all_gather x1, waiting for transfers between devices, broadcast(): lax.all_gather(x, axis)  90.3 us
    another operation x13, other arithmetic, invert_lower(): factor = jnp.linalg.cholesky(block)  68.6 us
    all_gather x1, waiting for transfers between devices, on_device(): gathered = lax.all_gather(both, ROW, axis=0, tiled=True)  67.3 us
    psum x5, blocking collectives, by_axis(): x = lax.psum(x, axis)  60.7 us
    another operation x5, other arithmetic, invert_lower(): lax.linalg.triangular_solve(factor, identity, left_side=True, lower=True)  51.5 us
    all_to_all x2, blocking collectives, summed_on_arrival(): lax.all_to_all(blocks, axis, split_axis=0, concat_axis=0, tiled=True)  43.3 us
    all_to_all x2, waiting for transfers between devices, from_everyone(): lax.all_to_all(jnp.broadcast_to(x[None], (size, *x.shape)), axis, 0, 0, t...  27.1 us
  transfers between devices with their start and end apart: 6, of which 5 were waited for; matrix products, arithmetic and copies ran while one was open for 0% of the time, Pallas kernels for 0%

commit v1 on v0

--- a/solution.py
+++ b/solution.py
@@ -139,7 +139,8 @@
         column_two - product(lower_one, crossing.T), inverse_two, panel_size, row_ids, panel_size
     )
     both = jnp.concatenate([lower_one, lower_two], axis=1)
-    gathered = lax.all_gather(both, ROW, axis=0, tiled=True)
+    repeated = jnp.stack([both] * lax.axis_size(ROW))
+    gathered = jnp.concatenate(lax.all_to_all(repeated, ROW, 0, 0), axis=0)
     mine = lax.dynamic_slice_in_dim(gathered, lax.axis_index(COL) * tile_cols, tile_cols, 0)
     matrix = gram - product(both, mine.T)
     inverses = [inverse_one, inverse_two]

time: 590 us -> 718 us (1.22)
  waiting for transfers between devices: 284 us -> 399 us
    all_to_all x0 -> x1, waiting for transfers between devices: none -> 183 us  [on_device(): gathered = jnp.concatenate(lax.all_to_all(repeated, ROW, 0, 0), axis=0)]
    all_gather x1 -> x0, waiting for transfers between devices: 67.3 us -> none  [on_device(): gathered = lax.all_gather(both, ROW, axis=0, tiled=True)]
where the time goes in v1:
time: 718 us; the launch traced here: 711 us
  waiting for transfers between devices  399 us (56%)
  other arithmetic  123 us (17%)
  blocking collectives  104 us (14%)
  starting transfers between devices  27.6 us (4%)
  between operations  20.3 us (3%)
  local copies, waits for them, and re-layouts  18.4 us (3%)
  matrix products  18.1 us (3%)
    all_to_all x1, waiting for transfers between devices, on_device(): gathered = jnp.concatenate(lax.all_to_all(repeated, ROW, 0, 0), axis=0)  183 us
    all_gather x1, waiting for transfers between devices, on_device(): lax.all_gather(x_slab, ROW, axis=1, tiled=True)  98.4 us
    all_gather x1, waiting for transfers between devices, broadcast(): lax.all_gather(x, axis)  90.3 us
    another operation x13, other arithmetic, invert_lower(): factor = jnp.linalg.cholesky(block)  68.6 us
    psum x5, blocking collectives, by_axis(): x = lax.psum(x, axis)  60.7 us
    another operation x5, other arithmetic, invert_lower(): lax.linalg.triangular_solve(factor, identity, left_side=True, lower=True)  51.5 us
    all_to_all x2, blocking collectives, summed_on_arrival(): lax.all_to_all(blocks, axis, split_axis=0, concat_axis=0, tiled=True)  43.3 us
    all_to_all x2, waiting for transfers between devices, from_everyone(): lax.all_to_all(jnp.broadcast_to(x[None], (size, *x.shape)), axis, 0, 0, t...  27.2 us
  transfers between devices with their start and end apart: 6, of which 5 were waited for; matrix products, arithmetic and copies ran while one was open for 0% of the time, Pallas kernels for 0%

profile of v1, /device:TPU:1, one launch (start us, length us, event | category | flops | bytes accessed | tf_op | source)
XLA Modules:
  0.0 710.9 jit_solution(11933141065230400715)
XLA Ops:
  7.2 0.7 all-gather.3.cloned.1.call-update
  7.9 98.4 %all-gather.3.cloned.1.call-done = f32[512,4096]{1,0:T(8,128)} async-done(((f32[512,128]{1,0:T(8,128)}), f32[512,4096]{1,0:T(8,128)}) %all-gather.3.cloned.1.call-update) | async-done | bytes 8388624 | tf_op jit(solution)/shard_map/all_gather | solution.py:119
  106.3 6.9 fusion.41
  113.2 1.6 copy.21
  114.8 9.5 %all-to-all-start = ((f32[16,128,256]{2,1,0:T(8,128)}), f32[16,128,256]{2,1,0:T(8,128)S(1)}, u32[]{:S(2)}, u32[]{:S(2)}) async-start(f32[16,128,256]{2,1,0:T(8,128)} %bitcast.101), calls=%async_computation | async-start | bytes 4194304 | tf_op jit(solution)/shard_map/all_to_all | solution.py:26
  124.4 0.7 multiply_reduce_fusion
  125.0 4.4 psum.35
  129.4 15.1 %psum.36 = f32[]{:T(128)} all-reduce(f32[]{:T(128)} %psum.35), channel_id=1, replica_groups=mesh['row_0'=2,'row_1'=8,'row_2'=2,'col_0'=8,'col_1'=2] {'row_1'}, use_global_device_ids=true, to_apply=%region_3.0 | all-reduce | flops 1 | bytes 8 | tf_op jit(solution)/shard_map/psum | solution.py:59
  144.5 6.4 psum.37
  151.0 28.8 %psum.38 = f32[]{:T(128)} all-reduce(f32[]{:T(128)} %psum.37), channel_id=1, replica_groups=mesh['row_0'=2,'row_1'=8,'row_2'=2,'col_0'=8,'col_1'=2] {'col_0'}, use_global_device_ids=true, to_apply=%region_5.0 | all-reduce | flops 1 | bytes 8 | tf_op jit(solution)/shard_map/psum | solution.py:59
  179.8 5.9 psum.39
  187.1 0.7 bitcast_add_fusion.2
  187.9 90.3 %all-gather.5.cloned.1.call-done = f32[16,128,256]{2,1,0:T(8,128)} async-done(((f32[1,128,256]{2,1,0:T(8,128)}), f32[16,128,256]{2,1,0:T(8,128)}) %all-gather.5.cloned.1.call-update) | async-done | bytes 2097168 | tf_op jit(solution)/shard_map/all_gather | solution.py:15
  278.2 1.2 fusion.10
  279.4 22.4 %all_to_all.35 = f32[32,8,256]{2,1,0:T(8,128)S(1)} all-to-all(f32[32,8,256]{2,1,0:T(8,128)S(1)} %fusion.10), channel_id=1, replica_groups=mesh['row_0'=2,'row_1'=8,'row_2'=2,'col_0'=8,'col_1'=2] {'row_0','row_1'..., dimensions={0} | all-to-all | bytes 524288 | tf_op jit(solution)/shard_map/all_to_all | solution.py:26
  301.8 0.7 broadcast_in_dim.4
  302.5 5.8 all-to-all-start.2
  308.4 1.2 fusion.8
  309.7 10.4 %all-to-all-done.2 = f32[32,8,256]{2,1,0:T(8,128)S(1)} async-done(((f32[32,8,256]{2,1,0:T(8,128)}), f32[32,8,256]{2,1,0:T(8,128)S(1)}, u32[]{:S(2)}, u32[]{:S(2)}) %all-to-all-start.2) | async-done | bytes 262176 | tf_op jit(solution)/shard_map/all_to_all | solution.py:43
  320.4 11.7 %cholesky.130 = f32[128,128]{1,0:T(8,128)S(1)} custom-call(f32[128,128]{1,0:T(8,128)S(1)} %cholesky.194), custom_call_target="Cholesky" | custom-call | tf_op jit(solution)/shard_map/jit(cholesky)/cholesky | solution.py:82
  332.1 9.8 %custom-call.13 = f32[1,128,128]{1,2,0:T(8,128)S(1)} custom-call(f32[1,128,128]{2,1,0:T(8,128)S(1)} %get-tuple-element.51), custom_call_target="InvertDiagBlocksLowerTriangular" | custom-call | tf_op jit(solution)/shard_map/jit(cholesky)/cholesky | solution.py:82
  342.4 11.7 %cholesky.147 = f32[128,128]{1,0:T(8,128)S(1)} custom-call(f32[128,128]{1,0:T(8,128)S(1)} %convolution_subtract_fusion.6), custom_call_target="Cholesky" | custom-call | tf_op jit(solution)/shard_map/jit(cholesky)/cholesky | solution.py:82
  354.2 0.6 compare_reduce_fusion.2
  356.2 4.0 while.4
  356.9 1.4 bitcast_dynamic-update-slice_fusion.4
  358.9 1.4 bitcast_dynamic-update-slice_fusion.4
  360.3 31.8 %custom-call.14 = f32[2,128,128]{1,2,0:T(8,128)S(1)} custom-call(f32[2,128,128]{2,1,0:T(8,128)S(1)} %get-tuple-element.20), custom_call_target="InvertDiagBlocksLowerTriangular" | custom-call | tf_op jit(solution)/shard_map/triangular_solve/custom-call.0 | solution.py:84
  393.0 1.3 convolution_select_fusion.1
  395.3 21.0 %all_to_all.36 = f32[32,1,4096]{2,1,0:T(1,128)S(1)} all-to-all(f32[32,1,4096]{2,1,0:T(1,128)S(1)} %all_to_all.25), channel_id=1, replica_groups=mesh['row_0'=2,'row_1'=8,'row_2'=2,'col_0'=8,'col_1'=2] {'row_0','row_1'..., dimensions={0} | all-to-all | bytes 1048576 | tf_op jit(solution)/shard_map/all_to_all | solution.py:26
  416.6 1.3 broadcast_in_dim.5
  417.9 5.6 all-to-all-start.4
  423.5 16.7 %all-to-all-done.4 = f32[32,1,4096]{2,1,0:T(1,128)S(1)} async-done(((f32[32,1,4096]{2,1,0:T(1,128)}), f32[32,1,4096]{2,1,0:T(1,128)S(1)}, u32[]{:S(2)}, u32[]{:S(2)}) %all-to-all-start.4) | async-done | bytes 524320 | tf_op jit(solution)/shard_map/all_to_all | solution.py:43
  440.2 1.3 slice_reduce_fusion
  442.4 11.7 %cholesky.164 = f32[128,128]{1,0:T(8,128)S(1)} custom-call(f32[128,128]{1,0:T(8,128)S(1)} %cholesky.197), custom_call_target="Cholesky" | custom-call | tf_op jit(solution)/shard_map/jit(cholesky)/cholesky | solution.py:82
  454.1 0.6 compare_reduce_fusion.1
  454.8 9.8 %custom-call.15 = f32[1,128,128]{1,2,0:T(8,128)S(1)} custom-call(f32[1,128,128]{2,1,0:T(8,128)S(1)} %get-tuple-element.47), custom_call_target="InvertDiagBlocksLowerTriangular" | custom-call | tf_op jit(solution)/shard_map/jit(cholesky)/cholesky | solution.py:82
  465.1 11.8 %cholesky.181 = f32[128,128]{1,0:T(8,128)S(1)} custom-call(f32[128,128]{1,0:T(8,128)S(1)} %convolution_subtract_fusion.5), custom_call_target="Cholesky" | custom-call | tf_op jit(solution)/shard_map/jit(cholesky)/cholesky | solution.py:82
  476.9 0.6 compare_reduce_fusion
  478.9 4.0 while.5
  479.5 1.4 bitcast_dynamic-update-slice_fusion.5
  481.5 1.4 bitcast_dynamic-update-slice_fusion.5
  482.9 19.7 %custom-call.16 = f32[2,128,128]{1,2,0:T(8,128)S(1)} custom-call(f32[2,128,128]{2,1,0:T(8,128)S(1)} %get-tuple-element.21), custom_call_target="InvertDiagBlocksLowerTriangular" | custom-call | tf_op jit(solution)/shard_map/triangular_solve/custom-call.0 | solution.py:84
  503.5 1.3 convolution_subtract_fusion.2
  505.3 4.3 stack.8
  509.6 6.6 all-to-all-start.5
  516.8 0.8 pad_maximum_fusion.1
  517.7 182.7 %all-to-all-done.5 = f32[32,128,512]{2,1,0:T(8,128)} async-done(((f32[32,128,512]{2,1,0:T(8,128)}), f32[32,128,512]{2,1,0:T(8,128)}, u32[]{:S(2)}, u32[]{:S(2)}) %all-to-all-start.5) | async-done | bytes 8388640 | tf_op jit(solution)/shard_map/all_to_all | solution.py:143
  700.3 2.4 convolution_subtract_fusion.1
  (65 shorter events, 8.5 us)
Async XLA Ops:
  7.2 99.1 %all-gather.3.cloned.1.call-start = ((), (), s32[]{:S(2)}) async-start(), calls=%async_computation.6 | async-start | bytes 8650752 | tf_op jit(solution)/shard_map/all_gather | solution.py:119
  114.8 9.6 %copy-start.1 = (f32[512,128]{1,0:T(8,128)S(1)}, f32[512,128]{1,0:T(8,128)}, u32[]{:S(2)}) copy-start(f32[512,128]{1,0:T(8,128)} %param.5) | copy-start | bytes 786436
  114.8 72.2 %all-to-all-start = ((f32[16,128,256]{2,1,0:T(8,128)}), f32[16,128,256]{2,1,0:T(8,128)S(1)}, u32[]{:S(2)}, u32[]{:S(2)}) async-start(f32[16,128,256]{2,1,0:T(8,128)} %bitcast.101), calls=%async_computation | async-start | bytes 4194304 | tf_op jit(solution)/shard_map/all_to_all | solution.py:26
  124.3 153.9 %all-gather.5.cloned.1.call-start = ((), (), s32[]{:S(2)}) async-start(), calls=%async_computation.7 | async-start | bytes 2228224 | tf_op jit(solution)/shard_map/all_gather | solution.py:15
  302.5 17.6 %all-to-all-start.2 = ((f32[32,8,256]{2,1,0:T(8,128)}), f32[32,8,256]{2,1,0:T(8,128)S(1)}, u32[]{:S(2)}, u32[]{:S(2)}) async-start(f32[32,8,256]{2,1,0:T(8,128)} %broadcast_in_dim.4), calls=%async_computation.2 | async-start | bytes 524288 | tf_op jit(solution)/shard_map/all_to_all | solution.py:43
  417.9 22.3 %all-to-all-start.4 = ((f32[32,1,4096]{2,1,0:T(1,128)}), f32[32,1,4096]{2,1,0:T(1,128)S(1)}, u32[]{:S(2)}, u32[]{:S(2)}) async-start(f32[32,1,4096]{2,1,0:T(1,128)} %broadcast_in_dim.5), calls=%async_computation.4 | async-start | bytes 1048576 | tf_op jit(solution)/shard_map/all_to_all | solution.py:43
  505.3 195.1 %copy-start = (f32[128,512]{1,0:T(8,128)}, f32[128,512]{1,0:T(8,128)S(1)}, u32[]{:S(2)}) copy-start(f32[128,512]{1,0:T(8,128)S(1)} %pad_maximum_fusion.4) | copy-start | bytes 786436
  509.6 190.8 %all-to-all-start.5 = ((f32[32,128,512]{2,1,0:T(8,128)}), f32[32,128,512]{2,1,0:T(8,128)}, u32[]{:S(2)}, u32[]{:S(2)}) async-start(f32[32,128,512]{2,1,0:T(8,128)} %stack.8), calls=%async_computation.5 | async-start | bytes 16777216 | tf_op jit(solution)/shard_map/all_to_all | solution.py:143
Sparse Core Ops, SparseCore 0:
  10.0 96.2 all-gather.2
  188.0 90.1 all-gather.4
